TPU v7x, 32 devices: a whole 2x2x4 slice. The times are simulated.
32 devices in a mesh: row: 8 (over y, x, core), col: 4 (over z).
Axes of the slice: x: 2, y: 2, z: 4, core: 2. Of those that a mesh axis runs over, the one named last changes fastest.
Arguments:
- src_points: bfloat16 [8192, 256], P('row'), may hold values from -32 to 32, as said below
- tgt_points: bfloat16 [16384, 256], P(('col', 'row')), may hold values from -32 to 32, as said below
- log_src_mass: float32 [8192], P('row'), may hold values from -3 to 3
- log_tgt_mass: float32 [16384], P('col'), may hold values from -3 to 3
Outputs:
- src_potential: float32 [8192], P('row')
- tgt_potential: float32 [16384], P('col')
- mean_potentials: float32 [], replicated
Inputs may be any that keep to these rules, and one draw needn't show every extreme that they name: `src_points`: point coordinates. `tgt_points`: point coordinates.
All inputs are finite; a program needn't handle non-finite values.
Results may differ from a plain program's by a relative error of at most 0.0003.
Values may be sent and summed in bfloat16 or wider, within the bound.
A program may use at most 64 MiB of HBM per device.

v0:
```python
import jax
import jax.numpy as jnp
from jax import lax
from jax.sharding import PartitionSpec as P

ITERS = 3
entropy_weight = 0.1


def combined_all(value, axis, combine):
    everything = jax.tree.map(lambda part: lax.all_gather(part, axis), value)
    leading = jax.tree.map(lambda part: part[0], everything)

    def turn(k, so_far):
        return combine(so_far, jax.tree.map(lambda part: part[k], everything))

    return lax.fori_loop(1, lax.axis_size(axis), turn, leading)


def cost_block(points_a, squares_a, points_b, squares_b):
    product = lax.dot_general(
        points_a, points_b, (((1,), (1,)), ((), ())), preferred_element_type=jnp.float32
    )
    return (squares_a[:, None] + squares_b[None, :] - 2.0 * product) / points_a.shape[1]


def combine(early, later):
    top = jnp.maximum(early[0], later[0])
    return (top, early[1] * jnp.exp(early[0] - top) + later[1] * jnp.exp(later[0] - top))


def body(src_points, tgt_points, log_src_mass, log_tgt_mass):
    targets = lax.all_gather(tgt_points, "row", axis=0, tiled=True)
    sqy = jnp.sum(targets.astype(jnp.float32) ** 2, axis=1)
    count = src_points.shape[0]
    block = min(256, count)
    blocks = count // block
    src_blocks = src_points.reshape(blocks, block, -1)
    sq_blocks = jnp.sum(src_points.astype(jnp.float32) ** 2, axis=1).reshape(blocks, block)
    mass_blocks = log_src_mass.reshape(blocks, block)
    width_tgt = targets.shape[0]
    tgt_potential = jnp.zeros((width_tgt,), jnp.float32)
    src_potential = jnp.zeros((count,), jnp.float32)
    for step in range(ITERS):

        def row_terms(points, squares):
            cost = cost_block(points, squares, targets, sqy)
            return log_tgt_mass[None, :] + (tgt_potential[None, :] - cost) / entropy_weight

        def row_pair(item):
            terms = row_terms(item[0], item[1])
            top = jnp.max(terms, axis=1)
            return (top, jnp.sum(jnp.exp(terms - top[:, None]), axis=1))

        top, total = lax.map(row_pair, (src_blocks, sq_blocks))
        top, total = combined_all((top.reshape(-1), total.reshape(-1)), "col", combine)
        src_potential = -entropy_weight * (top + jnp.log(total))
        pot_blocks = src_potential.reshape(blocks, block)

        def col_terms(points, squares, mass, pot):
            cost = cost_block(points, squares, targets, sqy)
            return mass[:, None] + (pot[:, None] - cost) / entropy_weight

        def pair_step(carry, item):
            terms = col_terms(item[0], item[1], item[2], item[3])
            block_top = jnp.max(terms, axis=0)
            block_sum = jnp.sum(jnp.exp(terms - block_top[None, :]), axis=0)
            return (combine(carry, (block_top, block_sum)), None)

        start = (
            jnp.full((width_tgt,), -jnp.inf, jnp.float32),
            jnp.zeros((width_tgt,), jnp.float32),
        )
        inputs = (src_blocks, sq_blocks, mass_blocks, pot_blocks)
        (top, total), unused = lax.scan(pair_step, start, inputs)
        top, total = combined_all((top, total), "row", combine)
        tgt_potential = -entropy_weight * (top + jnp.log(total))
    sources_all = count * lax.axis_size("row")
    targets_all = width_tgt * lax.axis_size("col")
    local = jnp.sum(src_potential) / (sources_all * lax.axis_size("col")) + jnp.sum(
        tgt_potential
    ) / (targets_all * lax.axis_size("row"))
    mean_potentials = lax.psum(local, ("row", "col"))
    return (src_potential, tgt_potential, mean_potentials)


def solution(mesh):
    return jax.shard_map(
        body,
        mesh=mesh,
        in_specs=(P("row", None), P(("col", "row"), None), P("row"), P("col")),
        out_specs=(P("row"), P("col"), P()),
        check_vma=False,
    )
```

profile of v0, /device:TPU:0, one launch (start us, length us, event | category | flops | bytes accessed | tf_op | source)
XLA Modules:
  0.0 320.3 jit_solution(3803695196308315043)
XLA Ops:
  9.9 30.5 %all-gather.14.cloned.1.call-done = bf16[4096,256]{1,0:T(8,128)(2,1)} async-done(((bf16[512,256]{1,0:T(8,128)(2,1)}), bf16[4096,256]{1,0:T(8,128)(2,1)}) %all-gather.14.cloned.1.call-update) | async-done | bytes 2097168 | tf_op jit(solution)/shard_map/all_gather | solution.py:33
  42.6 15.6 %while.177 = (s32[]{:T(128)}, f32[4,256]{1,0:T(4,128)S(1)}, f32[4,256]{1,0:T(4,128)S(1)}, f32[4096]{0:T(1024)}, f32[4,256]{1,0:T(4,128)S(1)}, /*index=5*/f32[409...) while((s32[]{:T(128)}, f32[4,256]{1,0:T(4,128)S(1)}, ...), condition=%wide.region_5.6_spmd, body=%wide.region_2.5_spmd.sunk | while | flops 547356160 | bytes 10660465 | solution.py:55
  58.3 13.3 %all-gather.6 = f32[4,1,1024]{2,1,0:T(1,128)S(1)} all-gather(f32[1,1,1024]{2,1,0:T(1,128)S(1)} %reshape.89), channel_id=1, replica_groups=mesh['row'=8,'col'=4] {'col'}, dimensions={0}, use_global_device_ids=true | all-gather | bytes 20480 | tf_op jit(solution)/shard_map/all_gather | solution.py:11
  71.5 13.2 %all-gather.7 = f32[4,1,1024]{2,1,0:T(1,128)S(1)} all-gather(f32[1,1,1024]{2,1,0:T(1,128)S(1)} %reshape.91), channel_id=1, replica_groups=mesh['row'=8,'col'=4] {'col'}, dimensions={0}, use_global_device_ids=true | all-gather | bytes 20480 | tf_op jit(solution)/shard_map/all_gather | solution.py:11
  85.0 15.2 %while.186 = (s32[]{:T(128)}, f32[4096]{0:T(1024)S(1)}, f32[4096]{0:T(1024)S(1)}, f32[4,256]{1,0:T(4,128)S(1)}, f32[4,256]{1,0:T(4,128)S(1)}, /*index=5*/f32[4,2...) while((s32[]{:T(128)}, f32[4096]{0:T(1024)S(1)}, ...), condition=%wide.region_11.12_spmd.clone, body=%wide.region_8.11_spmd.clone.sunk | while | flops 547381248 | bytes 10790527 | solution.py:75
  100.2 9.2 %all-gather = f32[32768]{0:T(1024)S(1)} all-gather(f32[4096]{0:T(1024)S(1)} %get-tuple-element.1088), channel_id=2, replica_groups=mesh['row'=8,'col'=4] {'row'}, dimensions={0}, use_global_device_ids=true | all-gather | bytes 147456 | tf_op jit(solution)/shard_map/all_gather | solution.py:11
  109.4 8.3 %all-gather.1 = f32[32768]{0:T(1024)S(1)} all-gather(f32[4096]{0:T(1024)S(1)} %get-tuple-element.1089), channel_id=3, replica_groups=mesh['row'=8,'col'=4] {'row'}, dimensions={0}, use_global_device_ids=true | all-gather | bytes 147456 | tf_op jit(solution)/shard_map/all_gather | solution.py:11
  118.3 16.0 %while.180 = (s32[]{:T(128)}, f32[4,256]{1,0:T(4,128)S(1)}, f32[4,256]{1,0:T(4,128)S(1)}, f32[4096]{0:T(1024)S(1)}, f32[4096]{0:T(1024)S(1)}, /*index=5*/f32[4,2...) while((s32[]{:T(128)}, f32[4,256]{1,0:T(4,128)S(1)}, ...), condition=%wide.region_17.18_spmd, body=%wide.region_14.17_spmd.sunk | while | flops 547356160 | bytes 10676857 | solution.py:55
  118.4 3.2 fusion.83
  126.4 3.2 fusion.83
  130.4 3.2 fusion.83
  134.4 13.2 %all-gather.8 = f32[4,1,1024]{2,1,0:T(1,128)S(1)} all-gather(f32[1,1,1024]{2,1,0:T(1,128)S(1)} %reshape.93), channel_id=1, replica_groups=mesh['row'=8,'col'=4] {'col'}, dimensions={0}, use_global_device_ids=true | all-gather | bytes 20480 | tf_op jit(solution)/shard_map/all_gather | solution.py:11
  147.6 13.2 %all-gather.9 = f32[4,1,1024]{2,1,0:T(1,128)S(1)} all-gather(f32[1,1,1024]{2,1,0:T(1,128)S(1)} %reshape.95), channel_id=1, replica_groups=mesh['row'=8,'col'=4] {'col'}, dimensions={0}, use_global_device_ids=true | all-gather | bytes 20480 | tf_op jit(solution)/shard_map/all_gather | solution.py:11
  161.0 15.2 %while.187 = (s32[]{:T(128)}, f32[4096]{0:T(1024)S(1)}, f32[4096]{0:T(1024)S(1)}, f32[4,256]{1,0:T(4,128)S(1)}, f32[4,256]{1,0:T(4,128)S(1)}, /*index=5*/f32[4,2...) while((s32[]{:T(128)}, f32[4096]{0:T(1024)S(1)}, ...), condition=%wide.region_23.24_spmd.clone, body=%wide.region_20.23_spmd.clone.sunk | while | flops 547381248 | bytes 10790527 | solution.py:75
  176.2 9.3 %all-gather.2 = f32[32768]{0:T(1024)S(1)} all-gather(f32[4096]{0:T(1024)S(1)} %get-tuple-element.1096), channel_id=4, replica_groups=mesh['row'=8,'col'=4] {'row'}, dimensions={0}, use_global_device_ids=true | all-gather | bytes 147456 | tf_op jit(solution)/shard_map/all_gather | solution.py:11
  185.6 8.3 %all-gather.3 = f32[32768]{0:T(1024)S(1)} all-gather(f32[4096]{0:T(1024)S(1)} %get-tuple-element.1097), channel_id=5, replica_groups=mesh['row'=8,'col'=4] {'row'}, dimensions={0}, use_global_device_ids=true | all-gather | bytes 147456 | tf_op jit(solution)/shard_map/all_gather | solution.py:11
  194.5 16.0 %while.183 = (s32[]{:T(128)}, f32[4,256]{1,0:T(4,128)S(1)}, f32[4,256]{1,0:T(4,128)S(1)}, f32[4096]{0:T(1024)S(1)}, f32[4096]{0:T(1024)S(1)}, /*index=5*/f32[4,2...) while((s32[]{:T(128)}, f32[4,256]{1,0:T(4,128)S(1)}, ...), condition=%wide.region_29.30_spmd, body=%wide.region_26.29_spmd.sunk | while | flops 547356160 | bytes 10676857 | solution.py:55
  198.6 3.2 fusion.85
  210.6 13.2 %all-gather.10 = f32[4,1,1024]{2,1,0:T(1,128)S(1)} all-gather(f32[1,1,1024]{2,1,0:T(1,128)S(1)} %reshape.97), channel_id=1, replica_groups=mesh['row'=8,'col'=4] {'col'}, dimensions={0}, use_global_device_ids=true | all-gather | bytes 20480 | tf_op jit(solution)/shard_map/all_gather | solution.py:11
  223.8 13.2 %all-gather.11 = f32[4,1,1024]{2,1,0:T(1,128)S(1)} all-gather(f32[1,1,1024]{2,1,0:T(1,128)S(1)} %reshape.99), channel_id=1, replica_groups=mesh['row'=8,'col'=4] {'col'}, dimensions={0}, use_global_device_ids=true | all-gather | bytes 20480 | tf_op jit(solution)/shard_map/all_gather | solution.py:11
  238.4 15.2 %while.188 = (s32[]{:T(128)}, f32[4096]{0:T(1024)S(1)}, f32[4096]{0:T(1024)S(1)}, f32[4,256]{1,0:T(4,128)S(1)}, f32[4,256]{1,0:T(4,128)S(1)}, /*index=5*/f32[4,2...) while((s32[]{:T(128)}, f32[4096]{0:T(1024)S(1)}, ...), condition=%wide.region_35.36_spmd.clone, body=%wide.region_32.35_spmd.clone.sunk | while | flops 547381248 | bytes 10790527 | solution.py:75
  253.6 9.2 %all-gather.4 = f32[32768]{0:T(1024)S(1)} all-gather(f32[4096]{0:T(1024)S(1)} %get-tuple-element.1104), channel_id=6, replica_groups=mesh['row'=8,'col'=4] {'row'}, dimensions={0}, use_global_device_ids=true | all-gather | bytes 147456 | tf_op jit(solution)/shard_map/all_gather | solution.py:11
  262.8 8.3 %all-gather.5 = f32[32768]{0:T(1024)S(1)} all-gather(f32[4096]{0:T(1024)S(1)} %get-tuple-element.1105), channel_id=7, replica_groups=mesh['row'=8,'col'=4] {'row'}, dimensions={0}, use_global_device_ids=true | all-gather | bytes 147456 | tf_op jit(solution)/shard_map/all_gather | solution.py:11
  274.3 39.1 %psum.7 = f32[]{:T(128)} all-reduce(f32[]{:T(128)S(6)} %add.464), channel_id=1, replica_groups=mesh['row'=8,'col'=4] {'row','col'}, use_global_device_ids=true, to_apply=%region_40.41 | all-reduce | flops 1 | bytes 8 | tf_op jit(solution)/shard_map/psum | solution.py:83
  (243 shorter events, 90.9 us)
Async XLA Ops:
  7.2 33.2 %all-gather.14.cloned.1.call-start = ((), (), s32[]{:S(2)}) async-start(), calls=%async_computation | async-start | bytes 2359296 | tf_op jit(solution)/shard_map/all_gather | solution.py:33
  85.0 33.3 %copy-start.1 = (f32[4096]{0:T(1024)S(1)}, f32[4096]{0:T(1024)}, u32[]{:S(2)}) copy-start(f32[4096]{0:T(1024)} %get-tuple-element.2387) | copy-start | bytes 49156
  237.8 0.6 copy-start
Sparse Core Ops, SparseCore 0:
  9.9 30.4 all-gather.13
where the time goes:
time: 322 us; the launch traced here: 320 us
  blocking collectives  171 us (53%)
  matrix products  75.1 us (23%)
  waiting for transfers between devices  31.2 us (10%)
  other arithmetic  22 us (7%)
  between operations  15.7 us (5%)
  local copies, waits for them, and re-layouts  3.61 us (1%)
    all_gather x12, blocking collectives, combined_all(): everything = jax.tree.map(lambda part: lax.all_gather(part, axis), value)  132 us
    dot_general x24, matrix products, cost_block(): lax.dot_general(points_a, points_b, (((1,), (1,)), ((), ())), preferred_e...  75.1 us
    psum x1, blocking collectives, body(): mean_potentials = lax.psum(local, ('row', 'col'))  39.1 us
    all_gather x1, waiting for transfers between devices, body(): targets = lax.all_gather(tgt_points, 'row', axis=0, tiled=True)  30.5 us
    reduce_sum x12, other arithmetic, row_pair(): return (top, jnp.sum(jnp.exp(terms - top[:, None]), axis=1))  8.61 us
    reduce_sum x12, other arithmetic, pair_step(): block_sum = jnp.sum(jnp.exp(terms - block_top[None, :]), axis=0)  7.15 us
  transfers between devices with their start and end apart: 1, of which 1 were waited for; matrix products, arithmetic and copies ran while one was open for 1% of the time, Pallas kernels for 0%

commit v1 on v0

--- a/solution.py
+++ b/solution.py
@@ -30,7 +30,10 @@
 
 
 def body(src_points, tgt_points, log_src_mass, log_tgt_mass):
-    targets = lax.all_gather(tgt_points, "row", axis=0, tiled=True)
+    size = lax.axis_size("row")
+    pieces = jnp.stack([tgt_points for _ in range(size)])
+    pieces = lax.all_to_all(pieces, "row", split_axis=0, concat_axis=0)
+    targets = jnp.concatenate(pieces, axis=0)
     sqy = jnp.sum(targets.astype(jnp.float32) ** 2, axis=1)
     count = src_points.shape[0]
     block = min(256, count)

time: 322 us -> 268 us (0.83)
  matrix products: 75.1 us -> 35.4 us
  between operations: 15.7 us -> 2.4 us
  starting transfers between devices: 0.04 us -> 5.2 us
  waiting for transfers between devices: 31.2 us -> 26.3 us
    dot_general x24, matrix products: 75.1 us -> 35.4 us  [cost_block(): lax.dot_general(points_a, points_b, (((1,), (1,)), ((), ())), preferred_e...]
    all_gather x1 -> x0, waiting for transfers between devices: 30.5 us -> none  [body(): targets = lax.all_gather(tgt_points, 'row', axis=0, tiled=True)]
    all_to_all x0 -> x1, waiting for transfers between devices: none -> 26.3 us  [body(): pieces = lax.all_to_all(pieces, 'row', split_axis=0, concat_axis=0)]
    all_to_all x0 -> x1, starting transfers between devices: none -> 5.2 us  [body(): pieces = lax.all_to_all(pieces, 'row', split_axis=0, concat_axis=0)]
  transfers between devices with their start and end apart: 1 -> 1, of which waited for: 1 -> 1; matrix products, arithmetic and copies ran while one was open for 1% -> 0% of each run, Pallas kernels for 0% -> 0%
where the time goes in v1:
time: 268 us; the launch traced here: 267 us
  blocking collectives  171 us (64%)
  matrix products  35.4 us (13%)
  waiting for transfers between devices  26.3 us (10%)
  other arithmetic  19.3 us (7%)
  local copies, waits for them, and re-layouts  5.42 us (2%)
  starting transfers between devices  5.2 us (2%)
    all_gather x12, blocking collectives, combined_all(): everything = jax.tree.map(lambda part: lax.all_gather(part, axis), value)  132 us
    psum x1, blocking collectives, body(): mean_potentials = lax.psum(local, ('row', 'col'))  39.3 us
    dot_general x24, matrix products, cost_block(): lax.dot_general(points_a, points_b, (((1,), (1,)), ((), ())), preferred_e...  35.4 us
    all_to_all x1, waiting for transfers between devices, body(): pieces = lax.all_to_all(pieces, 'row', split_axis=0, concat_axis=0)  26.3 us
    reduce_sum x12, other arithmetic, row_pair(): return (top, jnp.sum(jnp.exp(terms - top[:, None]), axis=1))  8.61 us
    reduce_sum x12, other arithmetic, pair_step(): block_sum = jnp.sum(jnp.exp(terms - block_top[None, :]), axis=0)  7.15 us
  transfers between devices with their start and end apart: 1, of which 1 were waited for; matrix products, arithmetic and copies ran while one was open for 0% of the time, Pallas kernels for 0%

profile of v1, /device:TPU:0, one launch (start us, length us, event | category | flops | bytes accessed | tf_op | source)
XLA Modules:
  0.0 267.1 jit_solution(7850110872487817237)
XLA Ops:
  0.7 2.5 stack.2
  3.2 5.2 %all-to-all-start = ((bf16[8,512,256]{2,1,0:T(8,128)(2,1)}), bf16[8,512,256]{2,1,0:T(8,128)(2,1)S(1)}, u32[]{:S(2)}, u32[]{:S(2)}) async-start(bf16[8,512,256]{2,1,0:T(8,128)(2,1)} %stack.2), calls=%async_computation | async-start | bytes 4194304 | tf_op jit(solution)/shard_map/all_to_all | solution.py:35
  8.7 26.3 %all-to-all-done = bf16[8,512,256]{2,1,0:T(8,128)(2,1)S(1)} async-done(((bf16[8,512,256]{2,1,0:T(8,128)(2,1)}), bf16[8,512,256]{2,1,0:T(8,128)(2,1)S(1)}, u32[]{:S(2)}, u32[]{:S(2)}) %all-to-all-start) | async-done | bytes 2097184 | tf_op jit(solution)/shard_map/all_to_all | solution.py:35
  35.6 9.3 %while.177 = (s32[]{:T(128)}, f32[4,256]{1,0:T(4,128)S(1)}, f32[4,256]{1,0:T(4,128)S(1)}, f32[4096]{0:T(1024)S(1)}, f32[4,256]{1,0:T(4,128)S(1)}, /*index=5*/f32...) while((s32[]{:T(128)}, f32[4,256]{1,0:T(4,128)S(1)}, ...), condition=%wide.region_5.6_spmd, body=%wide.region_2.5_spmd.sunk | while | flops 547356160 | bytes 10659957 | solution.py:58
  44.9 13.4 %all-gather.6 = f32[4,1,1024]{2,1,0:T(1,128)S(1)} all-gather(f32[1,1,1024]{2,1,0:T(1,128)S(1)} %reshape.96), channel_id=1, replica_groups=mesh['row'=8,'col'=4] {'col'}, dimensions={0}, use_global_device_ids=true | all-gather | bytes 20480 | tf_op jit(solution)/shard_map/all_gather | solution.py:11
  58.4 13.2 %all-gather.7 = f32[4,1,1024]{2,1,0:T(1,128)S(1)} all-gather(f32[1,1,1024]{2,1,0:T(1,128)S(1)} %reshape.98), channel_id=1, replica_groups=mesh['row'=8,'col'=4] {'col'}, dimensions={0}, use_global_device_ids=true | all-gather | bytes 20480 | tf_op jit(solution)/shard_map/all_gather | solution.py:11
  71.8 8.5 %while.186 = (s32[]{:T(128)}, f32[4096]{0:T(1024)S(1)}, f32[4096]{0:T(1024)S(1)}, f32[4,256]{1,0:T(4,128)S(1)}, f32[4,256]{1,0:T(4,128)S(1)}, /*index=5*/f32[4,2...) while((s32[]{:T(128)}, f32[4096]{0:T(1024)S(1)}, ...), condition=%wide.region_11.12_spmd.clone, body=%wide.region_8.11_spmd.clone.sunk | while | flops 547381248 | bytes 10790019 | solution.py:78
  80.3 8.3 %all-gather = f32[32768]{0:T(1024)S(1)} all-gather(f32[4096]{0:T(1024)S(1)} %get-tuple-element.1088), channel_id=2, replica_groups=mesh['row'=8,'col'=4] {'row'}, dimensions={0}, use_global_device_ids=true | all-gather | bytes 147456 | tf_op jit(solution)/shard_map/all_gather | solution.py:11
  88.6 9.2 %all-gather.1 = f32[32768]{0:T(1024)S(1)} all-gather(f32[4096]{0:T(1024)S(1)} %get-tuple-element.1089), channel_id=3, replica_groups=mesh['row'=8,'col'=4] {'row'}, dimensions={0}, use_global_device_ids=true | all-gather | bytes 147456 | tf_op jit(solution)/shard_map/all_gather | solution.py:11
  98.5 9.4 %while.180 = (s32[]{:T(128)}, f32[4,256]{1,0:T(4,128)S(1)}, f32[4,256]{1,0:T(4,128)S(1)}, f32[4096]{0:T(1024)S(1)}, f32[4096]{0:T(1024)S(1)}, /*index=5*/f32[4,2...) while((s32[]{:T(128)}, f32[4,256]{1,0:T(4,128)S(1)}, ...), condition=%wide.region_17.18_spmd, body=%wide.region_14.17_spmd.sunk | while | flops 547356160 | bytes 10676349 | solution.py:58
  107.8 13.2 %all-gather.8 = f32[4,1,1024]{2,1,0:T(1,128)S(1)} all-gather(f32[1,1,1024]{2,1,0:T(1,128)S(1)} %reshape.100), channel_id=1, replica_groups=mesh['row'=8,'col'=4] {'col'}, dimensions={0}, use_global_device_ids=true | all-gather | bytes 20480 | tf_op jit(solution)/shard_map/all_gather | solution.py:11
  121.1 13.2 %all-gather.9 = f32[4,1,1024]{2,1,0:T(1,128)S(1)} all-gather(f32[1,1,1024]{2,1,0:T(1,128)S(1)} %reshape.102), channel_id=1, replica_groups=mesh['row'=8,'col'=4] {'col'}, dimensions={0}, use_global_device_ids=true | all-gather | bytes 20480 | tf_op jit(solution)/shard_map/all_gather | solution.py:11
  134.5 8.5 %while.187 = (s32[]{:T(128)}, f32[4096]{0:T(1024)S(1)}, f32[4096]{0:T(1024)S(1)}, f32[4,256]{1,0:T(4,128)S(1)}, f32[4,256]{1,0:T(4,128)S(1)}, /*index=5*/f32[4,2...) while((s32[]{:T(128)}, f32[4096]{0:T(1024)S(1)}, ...), condition=%wide.region_23.24_spmd.clone, body=%wide.region_20.23_spmd.clone.sunk | while | flops 547381248 | bytes 10790019 | solution.py:78
  143.0 8.4 %all-gather.2 = f32[32768]{0:T(1024)S(1)} all-gather(f32[4096]{0:T(1024)S(1)} %get-tuple-element.1096), channel_id=4, replica_groups=mesh['row'=8,'col'=4] {'row'}, dimensions={0}, use_global_device_ids=true | all-gather | bytes 147456 | tf_op jit(solution)/shard_map/all_gather | solution.py:11
  151.5 9.2 %all-gather.3 = f32[32768]{0:T(1024)S(1)} all-gather(f32[4096]{0:T(1024)S(1)} %get-tuple-element.1097), channel_id=5, replica_groups=mesh['row'=8,'col'=4] {'row'}, dimensions={0}, use_global_device_ids=true | all-gather | bytes 147456 | tf_op jit(solution)/shard_map/all_gather | solution.py:11
  161.3 9.4 %while.183 = (s32[]{:T(128)}, f32[4,256]{1,0:T(4,128)S(1)}, f32[4,256]{1,0:T(4,128)S(1)}, f32[4096]{0:T(1024)S(1)}, f32[4096]{0:T(1024)S(1)}, /*index=5*/f32[4,2...) while((s32[]{:T(128)}, f32[4,256]{1,0:T(4,128)S(1)}, ...), condition=%wide.region_29.30_spmd, body=%wide.region_26.29_spmd.sunk | while | flops 547356160 | bytes 10676349 | solution.py:58
  163.7 1.5 fusion.85
  166.0 1.5 fusion.85
  170.7 13.2 %all-gather.10 = f32[4,1,1024]{2,1,0:T(1,128)S(1)} all-gather(f32[1,1,1024]{2,1,0:T(1,128)S(1)} %reshape.104), channel_id=1, replica_groups=mesh['row'=8,'col'=4] {'col'}, dimensions={0}, use_global_device_ids=true | all-gather | bytes 20480 | tf_op jit(solution)/shard_map/all_gather | solution.py:11
  184.0 13.2 %all-gather.11 = f32[4,1,1024]{2,1,0:T(1,128)S(1)} all-gather(f32[1,1,1024]{2,1,0:T(1,128)S(1)} %reshape.106), channel_id=1, replica_groups=mesh['row'=8,'col'=4] {'col'}, dimensions={0}, use_global_device_ids=true | all-gather | bytes 20480 | tf_op jit(solution)/shard_map/all_gather | solution.py:11
  198.6 8.4 %while.188 = (s32[]{:T(128)}, f32[4096]{0:T(1024)S(1)}, f32[4096]{0:T(1024)S(1)}, f32[4,256]{1,0:T(4,128)S(1)}, f32[4,256]{1,0:T(4,128)S(1)}, /*index=5*/f32[4,2...) while((s32[]{:T(128)}, f32[4096]{0:T(1024)S(1)}, ...), condition=%wide.region_35.36_spmd.clone, body=%wide.region_32.35_spmd.clone.sunk | while | flops 547381248 | bytes 10790019 | solution.py:78
  207.0 8.3 %all-gather.4 = f32[32768]{0:T(1024)S(1)} all-gather(f32[4096]{0:T(1024)S(1)} %get-tuple-element.1104), channel_id=6, replica_groups=mesh['row'=8,'col'=4] {'row'}, dimensions={0}, use_global_device_ids=true | all-gather | bytes 147456 | tf_op jit(solution)/shard_map/all_gather | solution.py:11
  215.3 9.2 %all-gather.5 = f32[32768]{0:T(1024)S(1)} all-gather(f32[4096]{0:T(1024)S(1)} %get-tuple-element.1105), channel_id=7, replica_groups=mesh['row'=8,'col'=4] {'row'}, dimensions={0}, use_global_device_ids=true | all-gather | bytes 147456 | tf_op jit(solution)/shard_map/all_gather | solution.py:11
  227.8 39.3 %psum.7 = f32[]{:T(128)} all-reduce(f32[]{:T(128)S(6)} %add.464), channel_id=1, replica_groups=mesh['row'=8,'col'=4] {'row','col'}, use_global_device_ids=true, to_apply=%region_40.41 | all-reduce | flops 1 | bytes 8 | tf_op jit(solution)/shard_map/psum | solution.py:86
  (248 shorter events, 56.8 us)
Async XLA Ops:
  0.6 7.8 %copy-start = (bf16[1024,256]{1,0:T(8,128)(2,1)S(1)}, bf16[1024,256]{1,0:T(8,128)(2,1)}, u32[]{:S(2)}) copy-start(bf16[1024,256]{1,0:T(8,128)(2,1)} %param.28) | copy-start | bytes 1572868
  0.6 8.0 %copy-start.2 = (f32[1024]{0:T(1024)S(1)}, f32[1024]{0:T(1024)}, u32[]{:S(2)}) copy-start(f32[1024]{0:T(1024)} %param.30) | copy-start | bytes 12292
  0.7 35.0 %copy-start.3 = (f32[4096]{0:T(1024)S(1)}, f32[4096]{0:T(1024)}, u32[]{:S(2)}) copy-start(f32[4096]{0:T(1024)} %param.31) | copy-start | bytes 49156
  3.2 31.8 %all-to-all-start = ((bf16[8,512,256]{2,1,0:T(8,128)(2,1)}), bf16[8,512,256]{2,1,0:T(8,128)(2,1)S(1)}, u32[]{:S(2)}, u32[]{:S(2)}) async-start(bf16[8,512,256]{2,1,0:T(8,128)(2,1)} %stack.2), calls=%async_computation | async-start | bytes 4194304 | tf_op jit(solution)/shard_map/all_to_all | solution.py:35
  198.0 0.6 copy-start.1
